TPU v7x, 256 devices: a 4x2x16 block of a 4x16x16 slice. The times are simulated.
256 devices in a mesh: cfg: 2 (over y), ta: 16 (over z), sa: 4 (over x), src: 2 (over core).
Axes of the slice: x: 4, y: 2, z: 16, core: 2. Of those that a mesh axis runs over, the one named last changes fastest.
The devices are a block of a 4x16x16 slice.
Arguments:
- prop: bfloat16 [4, 32, 2, 12, 12, 1024], P(('cfg', 'src'), 'ta', None, None, None, 'sa'), parts along dimension 0, may hold values from -6 to 6
- eps_rows: int32 [24, 3], replicated, may hold values from 0 to 11
- eps_sign: int32 [24], replicated, may hold values from 0 to 1
- source_sites: int32 [4, 3], P('cfg'), parts along dimension 0, may hold values from 0 to 15, as said below
- momenta: int32 [32, 3], replicated, may hold values from -2 to 2
Outputs:
- blocks: float32 [4, 32, 2, 32, 1728], P('cfg', None, None, 'ta', 'sa'), parts along dimension 0
There are 2 independent parts, one for each index of `cfg`. A program takes and returns all parts, laid end to end along the dimension named above; an argument that names none is the same for every part. Nothing has to cross between parts.
Inputs may be any that keep to these rules, and one draw needn't show every extreme that they name: `source_sites`: each row is a lattice site: first coordinate below 4, second below 16, third below 16.
All inputs are finite; a program needn't handle non-finite values.
Results may differ from a plain program's by a relative error of at most 0.0045.
Values sent between devices are 32-bit elements; how exact they have to be, the bound alone decides.
A program may use at most 128 MiB of HBM per device.

v0:
```python
import math

import jax
import jax.numpy as jnp
from jax import lax
from jax.sharding import PartitionSpec as P

LY = 16
LZ = 16


def cut_along(shard, dim, size):
    shape = shard.shape
    pieces = shard.reshape(*shape[:dim], size, shape[dim] // size, *shape[dim + 1 :])
    return jnp.moveaxis(pieces, dim, 0)


def summed_on_arrival(shard, axis, dim):
    size = lax.axis_size(axis)
    pieces = lax.all_to_all(cut_along(shard, dim, size), axis, 0, 0, tiled=True)
    return jnp.sum(pieces, axis=0)


def phase_table(position, momenta, site_index, extent_x):
    coord_x = site_index // (LY * LZ)
    coord_y = site_index // LZ % LY
    coord_z = site_index % LZ
    part_x = momenta[:, 0:1] * (coord_x[None, :] - position[0]) % extent_x
    part_y = momenta[:, 1:2] * (coord_y[None, :] - position[1]) % LY
    part_z = momenta[:, 2:3] * (coord_z[None, :] - position[2]) % LZ
    angle = (
        2.0
        * math.pi
        * (
            part_x.astype(jnp.float32) / extent_x
            + part_y.astype(jnp.float32) / LY
            + part_z.astype(jnp.float32) / LZ
        )
    )
    return jnp.concatenate([jnp.cos(angle), jnp.sin(angle)], axis=0).astype(jnp.bfloat16)


def contract(slab, rows, weights):
    first = jnp.take(slab, rows[:, 0], axis=1).astype(jnp.float32)
    second = jnp.take(slab, rows[:, 1], axis=1).astype(jnp.float32)
    third = jnp.take(slab, rows[:, 2], axis=1)
    scaled = weights[:, None, None, None]
    real = scaled * (
        first[0][:, :, None] * second[0][:, None] - first[1][:, :, None] * second[1][:, None]
    )
    imag = scaled * (
        first[0][:, :, None] * second[1][:, None] + first[1][:, :, None] * second[0][:, None]
    )
    pair = jnp.stack([real, imag]).astype(jnp.bfloat16)
    mixer = jnp.stack([jnp.stack([third[0], -third[1]]), jnp.stack([third[1], third[0]])])
    block = jnp.einsum("ceijx,oceLx->oijLx", pair, mixer, preferred_element_type=jnp.float32)
    width = slab.shape[1]
    return block.astype(jnp.bfloat16).reshape(2 * width * width * width, slab.shape[-1])


def mix_phase(table, quark):
    product = lax.dot_general(
        table, quark, (((1,), (1,)), ((), ())), preferred_element_type=jnp.float32
    )
    half_m = table.shape[0] // 2
    half_k = quark.shape[0] // 2
    cos_re = product[:half_m, :half_k]
    cos_im = product[:half_m, half_k:]
    sin_re = product[half_m:, :half_k]
    sin_im = product[half_m:, half_k:]
    return jnp.stack([cos_re + sin_im, cos_im - sin_re])


def per_device(prop, eps_rows, eps_sign, source_sites, momenta):
    src_count = prop.shape[0]
    time_count = prop.shape[1]
    width = prop.shape[3]
    site_count = prop.shape[5]
    sites_total = site_count * lax.axis_size("sa")
    extent_x = sites_total // (LY * LZ)
    site_index = lax.axis_index("sa") * site_count + jnp.arange(site_count, dtype=jnp.int32)
    weights = (2 * eps_sign - 1).astype(jnp.float32)
    scale = 1.0 / math.sqrt(4.0 * eps_rows.shape[0] * sites_total)
    first_source = lax.axis_index("src") * src_count
    positions = lax.dynamic_slice_in_dim(source_sites, first_source, src_count, 0)
    tables = jnp.stack([phase_table(positions[0], momenta, site_index, extent_x)])
    slabs = prop.reshape((src_count * time_count,) + prop.shape[2:])
    owners = jnp.repeat(jnp.arange(src_count, dtype=jnp.int32), time_count)

    def project(items):
        slab, owner = items
        quark = contract(slab, eps_rows, weights)
        return scale * mix_phase(tables[owner], quark)

    partial_value = lax.map(project, (slabs, owners))
    partial_value = partial_value.reshape(
        src_count, time_count, 2, momenta.shape[0], width * width * width
    )
    summed = summed_on_arrival(partial_value, "sa", 4)
    finished = lax.all_to_all(summed, "ta", split_axis=3, concat_axis=1, tiled=True)
    return lax.all_gather(finished, "src", axis=0, tiled=True)


def solution(mesh):
    return jax.shard_map(
        per_device,
        mesh=mesh,
        in_specs=(P(("cfg", "src"), "ta", None, None, None, "sa"), P(), P(), P("cfg", None), P()),
        out_specs=P("cfg", None, None, "ta", "sa"),
        check_vma=False,
    )
```

profile of v0, /device:TPU:33, one launch (start us, length us, event | category | flops | bytes accessed | tf_op | source)
XLA Modules:
  0.0 328.7 jit_solution(13275330639775343607)
XLA Ops:
  3.4 1.3 fusion.20
  5.6 254.8 %while.10 = (s32[]{:T(128)}, f32[2,2,32,1728]{3,2,1,0:T(8,128)}, bf16[2,2,12,12,256]{4,1,3,2,0:T(2,128)(2,1)}, s32[24,3]{0,1:T(4,128)}, f32[24]{0:T(128)S(1)}, /*index=5*/bf16[1,64,256]{2,1,0:T(8,128)(2,1)}, s32[]{:T(128)}) while((s32[]{:T(128)}, f32[2,2,32,1728]{3,2,1,0:T(8,128)}, bf16[2,2,12,12,256]{4,1,3,2,0:T(2,128)(2,1)}, ...), condition=%wide.region_1.3_spmd, body=%wide.region_0.2_spmd.sunk | while | flops 211418544 | bytes 58750516 | solution.py:95
  5.6 0.8 compare_and_fusion.4
  6.4 1.0 dynamic-slice_bitcast_fusion.2
  7.4 1.1 gather_fusion.1
  8.6 1.1 gather_fusion.2
  11.5 1.3 multiply_convert_fusion.3
  13.2 34.0 %copy.100 = bf16[2,24,12,12,256,1]{1,3,0,2,5,4:T(8,128)(2,1)} copy(bf16[2,24,12,12,256,1]{4,1,3,2,0,5:T(8,128)(2,1)S(1)} %maximum_bitcast_fusion.9) | data formatting | bytes 7077888 | tf_op jit(solution)/shard_map/while/body/eval_jaxpr/stack | solution.py:54
  47.2 2.0 gather_fusion
  50.6 6.5 %copy.95 = bf16[2,2,24,12,256,1]{2,3,1,5,0,4:T(8,128)(2,1)} copy(bf16[2,2,24,12,256,1]{4,2,3,1,0,5:T(8,128)(2,1)S(1)} %maximum_bitcast_fusion.8) | data formatting | bytes 1179648 | tf_op jit(solution)/shard_map/while/body/eval_jaxpr/stack | solution.py:55
  57.2 41.2 %fusion.48 = bf16[2,12,12,12,256]{2,3,1,0,4:T(8,128)(2,1)} fusion(bf16[2,2,24,12,256,1]{2,3,1,5,0,4:T(8,128)(2,1)} %copy.95, bf16[2,24,12,12,256,1]{1,3,0,2,5,4:T(8,128)(2,1)} %copy.100), kind=kOutput, calls=%fused_computation.4.clone.1 | convolution fusion | flops 85819392 | bytes 5898240 | tf_op jit(solution)/shard_map/while/body/eval_jaxpr/ceijx,oceLx->oijLx/dot_general | solution.py:56
  98.4 29.3 %copy.101 = bf16[2,12,12,12,256]{4,3,2,1,0:T(8,128)(2,1)S(1)} copy(bf16[2,12,12,12,256]{2,3,1,0,4:T(8,128)(2,1)} %fusion.48) | data formatting | bytes 3538944 | tf_op jit(solution)/shard_map/while/body/eval_jaxpr/convert_element_type | solution.py:58
  127.7 1.9 reshape.460
  129.6 2.1 convolution_bitcast_fusion.2
  132.0 0.9 copy-done.5
  133.8 1.0 dynamic-slice_bitcast_fusion.2
  134.8 1.1 gather_fusion.1
  136.0 1.1 gather_fusion.2
  138.9 1.3 multiply_convert_fusion.3
  140.6 34.0 %copy.100 = bf16[2,24,12,12,256,1]{1,3,0,2,5,4:T(8,128)(2,1)} copy(bf16[2,24,12,12,256,1]{4,1,3,2,0,5:T(8,128)(2,1)S(1)} %maximum_bitcast_fusion.9) | data formatting | bytes 7077888 | tf_op jit(solution)/shard_map/while/body/eval_jaxpr/stack | solution.py:54
  174.6 2.0 gather_fusion
  178.0 6.5 %copy.95 = bf16[2,2,24,12,256,1]{2,3,1,5,0,4:T(8,128)(2,1)} copy(bf16[2,2,24,12,256,1]{4,2,3,1,0,5:T(8,128)(2,1)S(1)} %maximum_bitcast_fusion.8) | data formatting | bytes 1179648 | tf_op jit(solution)/shard_map/while/body/eval_jaxpr/stack | solution.py:55
  184.5 41.2 %fusion.48 = bf16[2,12,12,12,256]{2,3,1,0,4:T(8,128)(2,1)} fusion(bf16[2,2,24,12,256,1]{2,3,1,5,0,4:T(8,128)(2,1)} %copy.95, bf16[2,24,12,12,256,1]{1,3,0,2,5,4:T(8,128)(2,1)} %copy.100), kind=kOutput, calls=%fused_computation.4.clone.1 | convolution fusion | flops 85819392 | bytes 5898240 | tf_op jit(solution)/shard_map/while/body/eval_jaxpr/ceijx,oceLx->oijLx/dot_general | solution.py:56
  225.8 29.3 %copy.101 = bf16[2,12,12,12,256]{4,3,2,1,0:T(8,128)(2,1)S(1)} copy(bf16[2,12,12,12,256]{2,3,1,0,4:T(8,128)(2,1)} %fusion.48) | data formatting | bytes 3538944 | tf_op jit(solution)/shard_map/while/body/eval_jaxpr/convert_element_type | solution.py:58
  255.1 1.9 reshape.460
  257.0 2.1 convolution_bitcast_fusion.2
  259.4 0.9 copy-done.5
  260.3 2.4 reshape_reshape.3
  263.1 14.7 %all_to_all.23 = f32[4,1,2,2,32,432]{5,4,3,2,1,0:T(8,128)S(1)} all-to-all(f32[4,1,2,2,32,432]{5,4,3,2,1,0:T(8,128)S(1)} %copy.59), channel_id=1, replica_groups=mesh['cfg'=2,'ta'=16,'sa'=4,'src'=2] {'sa'}, dimensions={0} | all-to-all | bytes 1769472 | tf_op jit(solution)/shard_map/all_to_all | solution.py:20
  278.0 40.5 %all_to_all.24 = f32[1,2,2,32,432]{4,2,1,0,3:T(2,128)S(1)} all-to-all(f32[1,2,2,32,432]{4,2,1,0,3:T(2,128)S(1)} %copy.61), channel_id=1, replica_groups=mesh['cfg'=2,'ta'=16,'sa'=4,'src'=2] {'ta'}, dimensions={3} | all-to-all | bytes 442368 | tf_op jit(solution)/shard_map/all_to_all | solution.py:100
  318.8 8.7 %all_gather.3 = f32[2,32,2,2,432]{4,1,3,2,0:T(8,128)S(1)} all-gather(f32[1,32,2,2,432]{4,1,3,2,0:T(8,128)S(1)} %copy.64), channel_id=1, replica_groups=mesh['cfg'=2,'ta'=16,'sa'=4,'src'=2] {'src'}, dimensions={0}, use_global_device_ids=true | all-gather | bytes 663552 | tf_op jit(solution)/shard_map/all_gather | solution.py:101
  327.5 1.2 copy.65
  (73 shorter events, 13.3 us)
Async XLA Ops:
  0.0 0.7 copy-start
  7.4 4.1 %copy-start.2 = (bf16[2,12,12,256]{3,0,2,1:T(2,128)(2,1)}, bf16[2,12,12,256]{3,0,2,1:T(2,128)(2,1)S(1)}, u32[]{:S(2)}) copy-start(bf16[2,12,12,256]{3,0,2,1:T(2,128)(2,1)S(1)} %dynamic-slice_bitcast_fusion.2) | copy-start | bytes 442372 | tf_op jit(solution)/shard_map/while
  127.7 1.9 copy-start.3
  127.7 4.3 %copy-start.4 = (f32[2,2,32,1728]{3,2,1,0:T(8,128)S(1)}, f32[2,2,32,1728]{3,2,1,0:T(8,128)}, u32[]{:S(2)}) copy-start(f32[2,2,32,1728]{3,2,1,0:T(8,128)} %get-tuple-element.173) | copy-start | bytes 2654212 | tf_op jit(solution)/shard_map/while
  132.0 0.9 copy-start.5
  134.8 4.1 %copy-start.2 = (bf16[2,12,12,256]{3,0,2,1:T(2,128)(2,1)}, bf16[2,12,12,256]{3,0,2,1:T(2,128)(2,1)S(1)}, u32[]{:S(2)}) copy-start(bf16[2,12,12,256]{3,0,2,1:T(2,128)(2,1)S(1)} %dynamic-slice_bitcast_fusion.2) | copy-start | bytes 442372 | tf_op jit(solution)/shard_map/while
  255.0 1.9 copy-start.3
  255.0 4.3 %copy-start.4 = (f32[2,2,32,1728]{3,2,1,0:T(8,128)S(1)}, f32[2,2,32,1728]{3,2,1,0:T(8,128)}, u32[]{:S(2)}) copy-start(f32[2,2,32,1728]{3,2,1,0:T(8,128)} %get-tuple-element.173) | copy-start | bytes 2654212 | tf_op jit(solution)/shard_map/while
  259.4 0.9 copy-start.5
  262.7 66.0 %copy-start.1 = (s32[2,3]{1,0:T(2,128)S(1)}, s32[2,3]{1,0:T(2,128)}, u32[]{:S(2)}) copy-start(s32[2,3]{1,0:T(2,128)} %param.12) | copy-start | bytes 76
where the time goes:
time: 330 us; the launch traced here: 329 us
  local copies, waits for them, and re-layouts  165 us (50%)
  matrix products  86.7 us (26%)
  blocking collectives  63.8 us (19%)
  other arithmetic  12.5 us (4%)
    dot_general x2, matrix products, contract(): jnp.einsum('ceijx,oceLx->oijLx', pair, mixer, preferred_element_type=jnp....  82.4 us
    another operation x2, local copies, waits for them, and re-layouts, contract(): pair = jnp.stack([real, imag]).astype(jnp.bfloat16)  68 us
    convert_element_type x2, local copies, waits for them, and re-layouts, contract(): block.astype(jnp.bfloat16)  58.5 us
    all_to_all x1, blocking collectives, per_device(): lax.all_to_all(summed, 'ta', split_axis=3, concat_axis=1, tiled=True)  40.5 us
    all_to_all x1, blocking collectives, summed_on_arrival(): pieces = lax.all_to_all(cut_along(shard, dim, size), axis, 0, 0, tiled=True)  14.7 us
    another operation x2, local copies, waits for them, and re-layouts, contract(): jnp.stack([jnp.stack([third[0], -third[1]]), jnp.stack([third[1], third[0...  13.1 us
    all_gather x1, blocking collectives, per_device(): return lax.all_gather(finished, 'src', axis=0, tiled=True)  8.7 us

commit v1 on v0

v1 whole, which is shorter than its diff:
```python
import functools
import math

import jax
import jax.numpy as jnp
from jax import lax
from jax.experimental import pallas as pl
from jax.experimental.pallas import tpu as pltpu
from jax.sharding import PartitionSpec as P

LY = 16
LZ = 16
F32 = jnp.float32
BF16 = jnp.bfloat16
NT = (((1,), (1,)), ((), ()))


def split_rows(width, copies):
    rows = 2 * copies * width
    out = lax.broadcasted_iota(jnp.int32, (rows, 2 * width), 0)
    col = lax.broadcasted_iota(jnp.int32, (rows, 2 * width), 1)
    half = out // (copies * width)
    return (col == 2 * (out % width) + half).astype(F32).astype(BF16)


def group_kernel(terms, rows_ref, sign_ref, prop_ref, h_ref, f_ref, acc_ref):
    width = prop_ref.shape[1]
    sites = prop_ref.shape[3]
    spread = split_rows(width, 2)
    for r in range(width):
        both = jnp.dot(spread, prop_ref[0, r], preferred_element_type=F32)
        f_ref[r, 0] = both[: 2 * width]
        f_ref[r, 1] = both[2 * width :]
    acc_ref[...] = jnp.zeros_like(acc_ref)
    low = lax.broadcasted_iota(jnp.int32, (8, sites), 0) < 4

    def term(e, carry):
        r0, r1, r2 = rows_ref[0, e], rows_ref[1, e], rows_ref[2, e]
        w = (2 * sign_ref[0, e] - 1).astype(F32)
        re2 = [f_ref[r2, 0, 8 * k : 8 * k + 8, :] for k in range(3)]
        im2 = [f_ref[r2, 1, 8 * k : 8 * k + 8, :] for k in range(3)]
        for m in range(width // 2):
            re1 = [jnp.broadcast_to(f_ref[r1, 0, 2 * m + k : 2 * m + k + 1, :] * w, (8, sites)) for k in range(2)]
            im1 = [jnp.broadcast_to(f_ref[r1, 1, 2 * m + k : 2 * m + k + 1, :] * w, (8, sites)) for k in range(2)]
            re1 = [re1[0], jnp.where(low, re1[0], re1[1]), re1[1]]
            im1 = [im1[0], jnp.where(low, im1[0], im1[1]), im1[1]]
            for k in range(3):
                at = slice(24 * m + 8 * k, 24 * m + 8 * k + 8)
                acc_ref[r0, 0, at, :] += re1[k] * re2[k] - im1[k] * im2[k]
                acc_ref[r0, 1, at, :] += re1[k] * im2[k] + im1[k] * re2[k]
        return carry

    lax.fori_loop(0, terms, term, 0)
    for r in range(width):
        for c in range(2):
            h_ref[0, c, :, r * sites : (r + 1) * sites] = acc_ref[r, c].astype(BF16)


def cos16(k):
    k = k & 15
    k = jnp.minimum(k, 16 - k)
    out = jnp.full(k.shape, -1.0, F32)
    for n in range(8):
        out = jnp.where(k == n, F32(math.cos(math.pi * n / 8) if n != 4 else 0.0), out)
    return out.astype(BF16).astype(F32)


def column(row):
    n = row.shape[1]
    eye = lax.broadcasted_iota(jnp.int32, (n, n), 0) == lax.broadcasted_iota(jnp.int32, (n, n), 1)
    return jnp.sum(jnp.where(eye, jnp.broadcast_to(row.astype(F32), (n, n)), 0.0), axis=1, keepdims=True)


def phases(extent_x, mom_ref, site_ref, sites):
    mom = mom_ref.shape[1]
    src, sa = lax.axis_index("src"), lax.axis_index("sa")
    x = lax.broadcasted_iota(jnp.int32, (mom, sites), 1) + sa * sites
    where = (x // (LY * LZ), (x // LZ) % LY, x % LZ)
    total = jnp.zeros((mom, sites), jnp.int32)
    for d, extent in enumerate((extent_x, LY, LZ)):
        n = jnp.broadcast_to(column(mom_ref[d : d + 1, :]), (mom, sites)).astype(jnp.int32)
        total += (n * (where[d] - site_ref[src, d])) * (16 // extent)
    return cos16(total), cos16(total - 4)


def project(t, scale, prop_ref, h_ref, cos_ref, sin_ref, pf_ref, z_ref, v_ref, x_ref):
    width, sites = prop_ref.shape[1], prop_ref.shape[3]
    mom = cos_ref.shape[0]
    nsa, nta = x_ref.shape[1], x_ref.shape[2]
    third = width // nsa
    block = width * width
    spread = split_rows(width, 1)
    half = width * mom

    def one_row(r, carry):
        both = jnp.dot(spread, prop_ref[t, r], preferred_element_type=F32)
        at = pl.ds(pl.multiple_of(r * sites, sites), sites)
        cos, sin = cos_ref[...], sin_ref[...]
        for i in range(width):
            re, im = both[i : i + 1, :], both[width + i : width + i + 1, :]
            row = (i % third) * nsa * mom + (i // third) * mom
            pf_ref[row : row + mom, at] = (cos * re + sin * im).astype(BF16)
            pf_ref[half + row : half + row + mom, at] = (cos * im - sin * re).astype(BF16)
        return carry

    lax.fori_loop(0, width, one_row, 0)
    for c in range(2):
        z_ref[c] = lax.dot_general(pf_ref[...], h_ref[t, c], NT, preferred_element_type=F32)
    part = nsa * mom
    for c in range(2):
        for i in range(third):
            a, b = slice(i * part, (i + 1) * part), slice(half + i * part, half + (i + 1) * part)
            if c == 0:
                value = (z_ref[0, a, :] - z_ref[1, b, :]) * scale
            else:
                value = (z_ref[1, a, :] + z_ref[0, b, :]) * scale
            v_ref[:, i * block : (i + 1) * block] = value
        for s in range(nsa):
            x_ref[t, s, :, c] = v_ref[s * mom : (s + 1) * mom, :].reshape(nta, mom // nta, third * block)


def exchange_kernel(extent_x, scale, site_ref, mom_ref, prop_ref, h_ref, out_ref, *scratch):
    (cos_ref, sin_ref, pf_ref, z_ref, v_ref, x_ref, got1, got2, keep, relay, red) = scratch[:11]
    (s1_send, s1_recv, s2_send, s2_recv, a_send, a_recv, f_send, f_recv) = scratch[11:]
    times, nsa, nta = x_ref.shape[0], x_ref.shape[1], x_ref.shape[2]
    ta, sa, src = lax.axis_index("ta"), lax.axis_index("sa"), lax.axis_index("src")
    flip = sa + 1 - 2 * (sa % 2)
    mirror = nsa - 1 - sa
    mates = (flip, mirror)
    other = 1 - src
    hop = nta // 2

    barrier = pltpu.get_barrier_semaphore()
    for mate in mates:
        pl.semaphore_signal(barrier, inc=1, device_id={"sa": mate})
    pl.semaphore_signal(barrier, inc=1, device_id={"src": other})

    def greet(k, carry):
        pl.semaphore_signal(barrier, inc=1, device_id={"ta": (ta + k) % nta})
        return carry

    lax.fori_loop(1, nta, greet, 0)

    cos, sin = phases(extent_x, mom_ref, site_ref, prop_ref.shape[3])
    cos_ref[...] = cos
    sin_ref[...] = sin

    def first(t, half, slot):
        mate = mates[half]
        dest = mate if slot == 0 else nsa - 1 - mate if half == 0 else mate + 1 - 2 * (mate % 2)
        return pltpu.make_async_remote_copy(
            src_ref=x_ref.at[t, dest, pl.ds(half * hop, hop)],
            dst_ref=got1.at[t, half, slot],
            send_sem=s1_send.at[t, half, slot],
            recv_sem=s1_recv.at[t, half, slot],
            device_id={"sa": mate},
        )

    def second(t, half):
        return pltpu.make_async_remote_copy(
            src_ref=relay.at[t, half],
            dst_ref=got2.at[t, half],
            send_sem=s2_send.at[t, half],
            recv_sem=s2_recv.at[t, half],
            device_id={"sa": mates[1 - half]},
        )

    def spread(t, k):
        to = (ta + k) % nta
        return pltpu.make_async_remote_copy(
            src_ref=red.at[t, to],
            dst_ref=out_ref.at[src, ta, t],
            send_sem=a_send.at[t, k],
            recv_sem=a_recv.at[t, k],
            device_id={"ta": to},
        )

    def forward(t, k):
        at = (ta + nta - k) % nta
        return pltpu.make_async_remote_copy(
            src_ref=out_ref.at[src, at, t],
            dst_ref=out_ref.at[src, at, t],
            send_sem=f_send.at[t, k],
            recv_sem=f_recv.at[t, k],
            device_id={"src": other},
        )

    def start_first(t):
        for half in range(2):
            for slot in (1, 0):
                first(t, half, slot).start()

    def start_second(t):
        for half in range(2):
            first(t, half, 1).wait_recv()
            relay[t, half] = x_ref[t, mates[1 - half], half * hop : (half + 1) * hop] + got1[t, half, 1]
            second(t, half).start()
        for half in range(2):
            first(t, half, 0).wait_recv()
            keep[t, half] = x_ref[t, sa, half * hop : (half + 1) * hop] + got1[t, half, 0]

    def start_spread(t):
        for half in range(2):
            second(t, half).wait_recv()
            red[t, half * hop : (half + 1) * hop] = keep[t, half] + got2[t, half]
        for k in order(nta):
            spread(t, k).start()
        out_ref[src, ta, t] = red[t, ta]
        forward(t, 0).start()

    def collect(t):
        for k in reversed(order(nta)):
            spread(t, k).wait_recv()
            forward(t, k).start()

    for t in range(times):
        project(t, scale, prop_ref, h_ref, cos_ref, sin_ref, pf_ref, z_ref, v_ref, x_ref)
        if t == 0:
            pl.semaphore_wait(barrier, nta + 2)
        start_first(t)
        if t >= 1:
            start_second(t - 1)
            start_spread(t - 1)
    start_second(times - 1)
    for t in range(times - 1):
        collect(t)
    start_spread(times - 1)
    collect(times - 1)
    for t in range(times):
        for half in range(2):
            first(t, half, 0).wait_send()
            first(t, half, 1).wait_send()
            second(t, half).wait_send()
        for k in range(nta):
            if k > 0:
                spread(t, k).wait_send()
            forward(t, k).wait()


def order(nta):
    return sorted(range(1, nta), key=lambda k: (-min(k, nta - k), k))


def solution(mesh):
    nta, nsa = mesh.shape["ta"], mesh.shape["sa"]

    def per_device(prop, eps_rows, eps_sign, source_sites, momenta):
        times, width, sites = prop.shape[1], prop.shape[3], prop.shape[5]
        mom, terms = momenta.shape[0], eps_rows.shape[0]
        extent_x = sites * nsa // (LY * LZ)
        scale = 1.0 / math.sqrt(4.0 * terms * sites * nsa)
        block = width * width
        depth = width * sites
        slabs = prop.transpose(0, 1, 3, 4, 2, 5).reshape(times, width, 2 * width, sites)
        smem = pl.BlockSpec(memory_space=pltpu.SMEM)
        vmem = pl.BlockSpec(memory_space=pltpu.VMEM)
        h = pl.pallas_call(
            functools.partial(group_kernel, terms),
            grid=(times,),
            out_shape=jax.ShapeDtypeStruct((times, 2, block, depth), BF16),
            in_specs=[smem, smem, pl.BlockSpec((1, width, 2 * width, sites), lambda t: (t, 0, 0, 0))],
            out_specs=pl.BlockSpec((1, 2, block, depth), lambda t: (t, 0, 0, 0)),
            scratch_shapes=[
                pltpu.VMEM((width, 2, 2 * width, sites), F32),
                pltpu.VMEM((width, 2, block, sites), F32),
            ],
        )(eps_rows.T, eps_sign.reshape(1, terms), slabs)
        tail = (2, mom // nta, block * width // nsa)
        dma = pltpu.SemaphoreType.DMA
        out = pl.pallas_call(
            functools.partial(exchange_kernel, extent_x, scale),
            out_shape=jax.ShapeDtypeStruct((2, nta, times) + tail, F32),
            in_specs=[smem, vmem, vmem, vmem],
            out_specs=vmem,
            scratch_shapes=[
                pltpu.VMEM((mom, sites), F32),
                pltpu.VMEM((mom, sites), F32),
                pltpu.VMEM((2 * width * mom, depth), BF16),
                pltpu.VMEM((2, 2 * width * mom, block), F32),
                pltpu.VMEM((nsa * mom, block * width // nsa), F32),
                pltpu.VMEM((times, nsa, nta) + tail, F32),
                pltpu.VMEM((times, 2, 2, nta // 2) + tail, F32),
                pltpu.VMEM((times, 2, nta // 2) + tail, F32),
                pltpu.VMEM((times, 2, nta // 2) + tail, F32),
                pltpu.VMEM((times, 2, nta // 2) + tail, F32),
                pltpu.VMEM((times, nta) + tail, F32),
                dma((times, 2, 2)),
                dma((times, 2, 2)),
                dma((times, 2)),
                dma((times, 2)),
                dma((times, nta)),
                dma((times, nta)),
                dma((times, nta)),
                dma((times, nta)),
            ],
            compiler_params=pltpu.CompilerParams(collective_id=0, has_side_effects=True),
        )(source_sites, momenta.T, slabs, h)
        return out.reshape(2, nta * times, *tail)

    return jax.shard_map(
        per_device,
        mesh=mesh,
        in_specs=(P(("cfg", "src"), "ta", None, None, None, "sa"), P(), P(), P("cfg", None), P()),
        out_specs=P("cfg", None, None, "ta", "sa"),
        check_vma=False,
    )
```

time: 330 us -> 73.3 us (0.22)
  local copies, waits for them, and re-layouts: 165 us -> 3.66 us
  matrix products: 86.7 us -> 0 us
  Pallas kernels: 0 us -> 69.4 us
  blocking collectives: 63.8 us -> 0 us
  other arithmetic: 12.5 us -> 0 us
    dot_general x4 -> x0, matrix products: 86.7 us -> none  [the longest x2 82.4 us: contract(): jnp.einsum('ceijx,oceLx->oijLx', pair, mixer, preferred_element_type=jnp....]
    another operation x5 -> x0, local copies, waits for them, and re-layouts: 83.4 us -> none  [the longest x2 68 us: contract(): pair = jnp.stack([real, imag]).astype(jnp.bfloat16)]
    pallas_call x0 -> x2, Pallas kernels: none -> 69.4 us  [the longest x1 62.7 us: per_device(): pl.pallas_call(functools.partial(exchange_kernel, extent_x, scale), out_s...]
    convert_element_type x2 -> x0, local copies, waits for them, and re-layouts: 58.5 us -> none  [contract(): block.astype(jnp.bfloat16)]
    all_to_all x2 -> x0, blocking collectives: 55.1 us -> none  [the longest x1 40.5 us: per_device(): lax.all_to_all(summed, 'ta', split_axis=3, concat_axis=1, tiled=True)]
    all_gather x1 -> x0, blocking collectives: 8.7 us -> none  [per_device(): return lax.all_gather(finished, 'src', axis=0, tiled=True)]
    gather x6 -> x0, local copies, waits for them, and re-layouts: 8.66 us -> none  [the longest x2 4.1 us: contract(): third = jnp.take(slab, rows[:, 2], axis=1)]
    another operation x10 -> x0, other arithmetic: 3.88 us -> none
where the time goes in v1:
time: 73.3 us; the launch traced here: 73 us
  Pallas kernels  69.4 us (95%)
  local copies, waits for them, and re-layouts  3.66 us (5%)
    pallas_call x1, Pallas kernels, per_device(): pl.pallas_call(functools.partial(exchange_kernel, extent_x, scale), out_s...  62.7 us
    pallas_call x1, Pallas kernels, per_device(): pl.pallas_call(functools.partial(group_kernel, terms), grid=(times,), out...  6.68 us
    unnamed x1, local copies, waits for them, and re-layouts  1.87 us
    reshape x1, local copies, waits for them, and re-layouts, per_device(): prop.transpose(0, 1, 3, 4, 2, 5).reshape(times, width, 2 * width, sites)  1.79 us

profile of v1, /device:TPU:33, one launch (start us, length us, event | category | flops | bytes accessed | tf_op | source)
XLA Modules:
  0.0 73.0 jit_solution(5740008418287895421)
XLA Ops:
  0.0 1.8 %reshape.9.prop_ref = bf16[2,12,24,256]{3,2,1,0:T(8,128)(2,1)} reshape(bf16[1,2,12,12,2,256]{5,4,3,2,1,0:T(2,128)(2,1)} %bitcast.6) | data formatting | bytes 589824 | tf_op jit(solution)/shard_map/reshape | solution.py:254
  1.8 6.7 %shard_map.55.h_ref = bf16[2,2,144,3072]{3,2,1,0:T(8,128)(2,1)} custom-call(s32[3,24]{1,0:T(4,128)} %bitcast.7, s32[1,24]{1,0:T(1,128)} %bitcast.9, bf16[2,12,24,256]{3,2,1,0:T(8,128)(2,1)} %reshape.9.prop_ref), custom_call_target="tpu_custom_call" | custom-call | tf_op jit(solution)/shard_map/pallas_call | solution.py:257
  8.5 62.7 %shard_map.56 = f32[2,16,2,2,2,432]{5,4,3,2,1,0:T(2,128)} custom-call(s32[2,3]{1,0:T(2,128)} %site_ref.1, s32[3,32]{1,0:T(4,128)} %bitcast.8, bf16[2,12,24,256]{3,2,1,0:T(8,128)(2,1)} %reshape.9.prop_ref, bf16[2,2,144,3072]{3,2,1,0:T(8,128)(2,1)} %shard_map.55.h_ref), custom_call_target="tpu_custom_call" | custom-call | tf_op jit(solution)/shard_map/pallas_call | solution.py:270
  71.2 1.9 %copy.7 = f32[2,32,2,2,432]{4,3,2,1,0:T(2,128)} copy(f32[2,32,2,2,432]{4,3,2,1,0:T(2,128)} %bitcast.5) | data formatting | bytes 884736

commit v2 on v1

v2 whole, which is shorter than its diff:
```python
import functools
import math

import jax
import jax.numpy as jnp
from jax import lax
from jax.experimental import pallas as pl
from jax.experimental.pallas import tpu as pltpu
from jax.sharding import PartitionSpec as P

LY = 16
LZ = 16
F32 = jnp.float32
BF16 = jnp.bfloat16
PARTS = 4
NT = (((1,), (1,)), ((), ()))


def split_rows(width, copies):
    rows = 2 * copies * width
    out = lax.broadcasted_iota(jnp.int32, (rows, 2 * width), 0)
    col = lax.broadcasted_iota(jnp.int32, (rows, 2 * width), 1)
    half = out // (copies * width)
    return (col == 2 * (out % width) + half).astype(F32).astype(BF16)


def load_rows(prop_ref, f_ref):
    times, width, _, _, sites = prop_ref.shape
    spread = split_rows(width, 2)
    for t in range(times):
        for r in range(width):
            rows = prop_ref[t, r].reshape(2 * width, sites)
            both = jnp.dot(spread, rows, preferred_element_type=F32)
            f_ref[t, r, 0] = both[: 2 * width]
            f_ref[t, r, 1] = both[2 * width :]


def add_terms(t, terms, rows_ref, sign_ref, f_ref, sum_ref):
    width, sites = f_ref.shape[1], f_ref.shape[4]
    low = lax.broadcasted_iota(jnp.int32, (8, sites), 0) < 4
    sum_ref[0] = jnp.zeros(sum_ref.shape[1:], F32)
    batch = 2

    def term(e, last):
        r0, r1, r2 = rows_ref[0, e], rows_ref[1, e], rows_ref[2, e]
        w = (2 * sign_ref[0, e] - 1).astype(F32)
        before = jnp.int32(0)
        for r in range(width):
            before = jnp.where(r0 == r, last[r], before)
        re2 = [f_ref[t, r2, 0, 8 * k : 8 * k + 8, :] * w for k in range(3)]
        im2 = [f_ref[t, r2, 1, 8 * k : 8 * k + 8, :] * w for k in range(3)]
        for m0 in range(0, width // 2, batch):
            tiles = [(m, k) for m in range(m0, m0 + batch) for k in range(3)]
            old = [[sum_ref[before, c, 24 * m + 8 * k : 24 * m + 8 * k + 8, :] for c in range(2)] for m, k in tiles]
            for m in range(m0, m0 + batch):
                one = [
                    [jnp.broadcast_to(f_ref[t, r1, c, 2 * m + k : 2 * m + k + 1, :], (8, sites)) for k in range(2)]
                    for c in range(2)
                ]
                re1, im1 = [[rows[0], jnp.where(low, rows[0], rows[1]), rows[1]] for rows in one]
                for k in range(3):
                    at = slice(24 * m + 8 * k, 24 * m + 8 * k + 8)
                    old_re, old_im = old[tiles.index((m, k))]
                    sum_ref[e + 1, 0, at, :] = old_re + (re1[k] * re2[k] - im1[k] * im2[k])
                    sum_ref[e + 1, 1, at, :] = old_im + (re1[k] * im2[k] + im1[k] * re2[k])
        return tuple(jnp.where(r0 == r, e + 1, last[r]) for r in range(width))

    return lax.fori_loop(0, terms, term, (jnp.int32(0),) * width)


def cos16(k):
    k = k & 15
    k = jnp.minimum(k, 16 - k)
    out = jnp.full(k.shape, -1.0, F32)
    for n in range(8):
        out = jnp.where(k == n, F32(math.cos(math.pi * n / 8) if n != 4 else 0.0), out)
    return out.astype(BF16).astype(F32)


def step(n, nta):
    return nta // 2 + ((n + 1) // 2) * (1 - 2 * (n % 2))


def column(row):
    count = row.shape[1]
    nta = lax.axis_size("ta")
    near = count // nta
    at = lax.broadcasted_iota(jnp.int32, (count, count), 0)
    place = (lax.axis_index("ta") + step(at // near, nta)) % nta * near + at % near
    pick = lax.broadcasted_iota(jnp.int32, (count, count), 1) == place
    return jnp.sum(jnp.where(pick, jnp.broadcast_to(row.astype(F32), (count, count)), 0.0), axis=1, keepdims=True)


def phases(extent_x, mom_ref, site_ref, sites):
    mom = mom_ref.shape[1]
    src, sa = lax.axis_index("src"), lax.axis_index("sa")
    x = lax.broadcasted_iota(jnp.int32, (mom, sites), 1) + sa * sites
    where = (x // (LY * LZ), (x // LZ) % LY, x % LZ)
    total = jnp.zeros((mom, sites), jnp.int32)
    for d, extent in enumerate((extent_x, LY, LZ)):
        n = jnp.broadcast_to(column(mom_ref[d : d + 1, :]), (mom, sites)).astype(jnp.int32)
        total += (n * (where[d] - site_ref[src, d])) * (16 // extent)
    return cos16(total), cos16(total - 4)


def project(t, g, rows, last, sum_ref, f_ref, cos_ref, sin_ref, pf_ref, h_ref, z_ref):
    width, sites = f_ref.shape[1], f_ref.shape[4]
    mom = cos_ref.shape[0]
    nsa = lax.axis_size("sa")
    third = width // nsa
    half = width * mom
    slot = g % 2
    cos, sin = cos_ref[...], sin_ref[...]
    for n in range(rows):
        r = g * rows + n
        at = slice(n * sites, (n + 1) * sites)
        for c in range(2):
            h_ref[slot, c, :, at] = sum_ref[last[r], c].astype(BF16)
        for i in range(width):
            re, im = f_ref[t, r, 0, i : i + 1, :], f_ref[t, r, 1, i : i + 1, :]
            row = (i % third) * nsa * mom + (i // third) * mom
            pf_ref[slot, row : row + mom, at] = (cos * re + sin * im).astype(BF16)
            pf_ref[slot, half + row : half + row + mom, at] = (cos * im - sin * re).astype(BF16)
    for c in range(2):
        more = lax.dot_general(pf_ref[slot], h_ref[slot, c], NT, preferred_element_type=F32)
        z_ref[c] = more if g == 0 else z_ref[c] + more


def arrange(t, scale, z_ref, v_ref, x_ref):
    nsa, nta, _, near, run = x_ref.shape[1:]
    block = z_ref.shape[2]
    half = z_ref.shape[1] // 2
    part = nsa * nta * near
    for c in range(2):
        for i in range(run // block):
            a, b = slice(i * part, (i + 1) * part), slice(half + i * part, half + (i + 1) * part)
            if c == 0:
                value = (z_ref[0, a, :] - z_ref[1, b, :]) * scale
            else:
                value = (z_ref[1, a, :] + z_ref[0, b, :]) * scale
            v_ref[:, i * block : (i + 1) * block] = value
        for s in range(nsa):
            x_ref[t, s, :, c] = v_ref[s * nta * near : (s + 1) * nta * near, :].reshape(nta, near, run)


def blocks_kernel(extent_x, terms, scale, *refs):
    given, out_ref, held, load_sem, scratch = refs[:5], refs[5], refs[6:11], refs[11], refs[12:]
    site_ref, rows_ref, sign_ref, mom_ref, prop_ref = held
    (cos_ref, sin_ref, f_ref, sum_ref, pf_ref, h_ref, z_ref, v_ref) = scratch[:8]
    (x_ref, got1, got2, relay, red) = scratch[8:13]
    (s1_send, s1_recv, s2_send, s2_recv, a_send, a_recv, f_send, f_recv) = scratch[13:]
    times, nsa, nta = x_ref.shape[0], x_ref.shape[1], x_ref.shape[2]
    width = prop_ref.shape[1]
    parts, hop = got2.shape[1], got2.shape[3]
    ta, sa, src = lax.axis_index("ta"), lax.axis_index("sa"), lax.axis_index("src")
    flip = sa + 1 - 2 * (sa % 2)
    mirror = nsa - 1 - sa
    mates = (flip, mirror)
    other = 1 - src

    barrier = pltpu.get_barrier_semaphore()
    for n in range(nta - 1):
        pl.semaphore_signal(barrier, inc=1, device_id={"ta": (ta + step(n, nta)) % nta})
    for mate in mates:
        pl.semaphore_signal(barrier, inc=1, device_id={"sa": mate})
    pl.semaphore_signal(barrier, inc=1, device_id={"src": other})

    def span(q, half):
        return slice((2 * q + half) * hop, (2 * q + half + 1) * hop)

    def first(t, q, half, slot):
        mate = mates[half]
        dest = mate if slot == 0 else nsa - 1 - mate if half == 0 else mate + 1 - 2 * (mate % 2)
        return pltpu.make_async_remote_copy(
            src_ref=x_ref.at[t, dest, span(q, half)],
            dst_ref=got1.at[t, q, half, slot],
            send_sem=s1_send.at[t, q, half, slot],
            recv_sem=s1_recv.at[t, q, half, slot],
            device_id={"sa": mate},
        )

    def second(t, q, half):
        return pltpu.make_async_remote_copy(
            src_ref=relay.at[t, q, half],
            dst_ref=got2.at[t, q, half],
            send_sem=s2_send.at[t, q, half],
            recv_sem=s2_recv.at[t, q, half],
            device_id={"sa": mates[1 - half]},
        )

    def spread(t, n):
        return pltpu.make_async_remote_copy(
            src_ref=red.at[t, n],
            dst_ref=out_ref.at[src, ta, t],
            send_sem=a_send.at[t, n],
            recv_sem=a_recv.at[t, n],
            device_id={"ta": (ta + step(n, nta)) % nta},
        )

    def forward(t, n):
        at = (ta + nta - step(n, nta)) % nta
        return pltpu.make_async_remote_copy(
            src_ref=out_ref.at[src, at, t],
            dst_ref=out_ref.at[src, at, t],
            send_sem=f_send.at[t, n],
            recv_sem=f_recv.at[t, n],
            device_id={"src": other},
        )

    def start_first(t, q):
        for slot in (1, 0):
            for half in range(2):
                first(t, q, half, slot).start()

    def start_second(t, q):
        for half in range(2):
            first(t, q, half, 1).wait_recv()
            relay[t, q, half] = x_ref[t, mates[1 - half], span(q, half)] + got1[t, q, half, 1]
            second(t, q, half).start()

    def start_spread(t, q):
        for half in range(2):
            first(t, q, half, 0).wait_recv()
            second(t, q, half).wait_recv()
            red[t, span(q, half)] = x_ref[t, sa, span(q, half)] + got1[t, q, half, 0] + got2[t, q, half]
            for n in range((2 * q + half) * hop, (2 * q + half + 1) * hop):
                if n < nta - 1:
                    spread(t, n).start()
                else:
                    out_ref[src, ta, t] = red[t, n]
                    forward(t, n).start()

    def collect(t):
        for n in range(nta - 1):
            spread(t, n).wait_recv()
            forward(t, n).start()

    loads = [pltpu.make_async_copy(a, b, load_sem.at[n]) for n, (a, b) in enumerate(zip(given, held))]
    for load in loads:
        load.start()
    for load in loads[:4]:
        load.wait()
    cos, sin = phases(extent_x, mom_ref, site_ref, prop_ref.shape[4])
    cos_ref[...] = cos
    sin_ref[...] = sin
    loads[4].wait()
    load_rows(prop_ref, f_ref)
    groups = 3
    for t in range(times):
        last = add_terms(t, terms, rows_ref, sign_ref, f_ref, sum_ref)
        if t == 1:
            pl.semaphore_wait(barrier, nta + 2)
            for q in range(parts):
                start_first(t - 1, q)
        for g in range(groups):
            project(t, g, width // groups, last, sum_ref, f_ref, cos_ref, sin_ref, pf_ref, h_ref, z_ref)
            if t > 0 and g == 1:
                start_second(t - 1, 0)
        if t > 0:
            for q in range(1, parts):
                start_second(t - 1, q)
        arrange(t, scale, z_ref, v_ref, x_ref)
        if t > 0:
            for q in range(parts):
                start_first(t, q)
            for q in range(parts):
                start_spread(t - 1, q)
    t = times - 1
    for q in range(parts):
        start_second(t, q)
        if q > 0:
            start_spread(t, q - 1)
    start_spread(t, parts - 1)
    for t in range(times):
        collect(t)
    for t in range(times):
        for q in range(parts):
            for half in range(2):
                first(t, q, half, 0).wait_send()
                first(t, q, half, 1).wait_send()
                second(t, q, half).wait_send()
        for n in range(nta):
            if n < nta - 1:
                spread(t, n).wait_send()
            forward(t, n).wait()


def solution(mesh):
    nta, nsa = mesh.shape["ta"], mesh.shape["sa"]

    def per_device(prop, eps_rows, eps_sign, source_sites, momenta):
        times, width, sites = prop.shape[1], prop.shape[3], prop.shape[5]
        mom, terms = momenta.shape[0], eps_rows.shape[0]
        extent_x = sites * nsa // (LY * LZ)
        scale = 1.0 / math.sqrt(4.0 * terms * sites * nsa)
        block = width * width
        slabs = prop.transpose(0, 1, 3, 4, 2, 5).reshape(times, width, width, 2, sites)
        tail = (2, mom // nta, block * width // nsa)
        rows = width // 3
        parts = PARTS if nta % (2 * PARTS) == 0 else 1
        hop = nta // (2 * parts)
        dma = pltpu.SemaphoreType.DMA
        out = pl.pallas_call(
            functools.partial(blocks_kernel, extent_x, terms, scale),
            out_shape=jax.ShapeDtypeStruct((2, nta, times) + tail, F32),
            in_specs=[pl.BlockSpec(memory_space=pltpu.HBM)] * 5,
            out_specs=pl.BlockSpec(memory_space=pltpu.VMEM),
            scratch_shapes=[
                pltpu.SMEM(source_sites.shape, jnp.int32),
                pltpu.SMEM((3, terms), jnp.int32),
                pltpu.SMEM((1, terms), jnp.int32),
                pltpu.VMEM((3, mom), jnp.int32),
                pltpu.VMEM(slabs.shape, BF16),
                dma((5,)),
                pltpu.VMEM((mom, sites), F32),
                pltpu.VMEM((mom, sites), F32),
                pltpu.VMEM((times, width, 2, 2 * width, sites), F32),
                pltpu.VMEM((terms + 1, 2, block, sites), F32),
                pltpu.VMEM((2, 2 * width * mom, rows * sites), BF16),
                pltpu.VMEM((2, 2, block, rows * sites), BF16),
                pltpu.VMEM((2, 2 * width * mom, block), F32),
                pltpu.VMEM((nsa * mom, block * width // nsa), F32),
                pltpu.VMEM((times, nsa, nta) + tail, F32),
                pltpu.VMEM((times, parts, 2, 2, hop) + tail, F32),
                pltpu.VMEM((times, parts, 2, hop) + tail, F32),
                pltpu.VMEM((times, parts, 2, hop) + tail, F32),
                pltpu.VMEM((times, nta) + tail, F32),
                dma((times, parts, 2, 2)),
                dma((times, parts, 2, 2)),
                dma((times, parts, 2)),
                dma((times, parts, 2)),
                dma((times, nta)),
                dma((times, nta)),
                dma((times, nta)),
                dma((times, nta)),
            ],
            compiler_params=pltpu.CompilerParams(
                collective_id=0, has_side_effects=True, vmem_limit_bytes=32 * 1024 * 1024
            ),
        )(source_sites, eps_rows.T, eps_sign.reshape(1, terms), momenta.T, slabs)
        return out.reshape(2, nta * times, *tail)

    return jax.shard_map(
        per_device,
        mesh=mesh,
        in_specs=(P(("cfg", "src"), "ta", None, None, None, "sa"), P(), P(), P("cfg", None), P()),
        out_specs=P("cfg", None, None, "ta", "sa"),
        check_vma=False,
    )
```

time: 73.3 us -> 54.4 us (0.74)
  Pallas kernels: 69.4 us -> 51.8 us
  local copies, waits for them, and re-layouts: 3.66 us -> 2.46 us
    pallas_call x2 -> x1, Pallas kernels: 69.4 us -> 51.8 us  [per_device(): pl.pallas_call(functools.partial(blocks_kernel, extent_x, terms, scale),...]
    reshape x1 -> x0, local copies, waits for them, and re-layouts: 1.79 us -> none  [per_device(): prop.transpose(0, 1, 3, 4, 2, 5).reshape(times, width, 2 * width, sites)]
    unnamed x1 -> x11, local copies, waits for them, and re-layouts: 1.87 us -> 2.46 us
where the time goes in v2:
time: 54.4 us; the launch traced here: 54.2 us
  Pallas kernels  51.8 us (95%)
  local copies, waits for them, and re-layouts  2.46 us (5%)
    pallas_call x1, Pallas kernels, per_device(): pl.pallas_call(functools.partial(blocks_kernel, extent_x, terms, scale),...  51.8 us
    unnamed x11, local copies, waits for them, and re-layouts  2.46 us

profile of v2, /device:TPU:33, one launch (start us, length us, event | category | flops | bytes accessed | tf_op | source)
XLA Modules:
  0.0 54.2 jit_solution(12799919155719682553)
XLA Ops:
  0.0 0.0 copy-start.2
  0.0 0.0 copy-start.1
  0.0 0.0 copy-start.3
  0.0 0.0 copy-start.4
  0.0 0.7 %copy-done.2 = s32[32,3]{0,1:T(4,128)S(1)} copy-done((s32[32,3]{0,1:T(4,128)S(1)}, s32[32,3]{0,1:T(4,128)}, u32[]{:S(2)}) %copy-start.2) | copy-done | bytes 408
  0.7 0.0 copy-done.1
  0.7 0.0 copy-done.3
  0.7 0.0 copy-done.4
  0.7 0.0 copy-start
  0.7 1.0 %copy-done = bf16[1,2,2,12,12,256]{5,2,4,3,1,0:T(2,128)(2,1)S(1)} copy-done((bf16[1,2,2,12,12,256]{5,2,4,3,1,0:T(2,128)(2,1)S(1)}, bf16[1,2,2,12,12,256]{5,2,4,3,1,0:T(2,128)(2,1)}, u32[]{:S(2)}) %copy-start) | copy-done | bytes 294936
  1.7 51.8 %shard_map.55 = f32[2,16,2,2,2,432]{5,4,3,2,1,0:T(2,128)S(1)} custom-call(s32[2,3]{1,0:T(2,128)S(1)} %copy-done.3, s32[3,24]{1,0:T(4,128)S(1)} %bitcast.9, s32[1,24]{1,0:T(1,128)S(1)} %bitcast.11, s32[3,32]{1,0:T(4,128)S(1)} %bitcast.10, bf16[2,12,12,2,256]{4,3,2,1,0:T(2,128)(2,1)S(1)} %bitcast.8), custom_call_target="tpu_custom_call" | custom-call | tf_op jit(solution)/shard_map/pallas_call | solution.py:303
  53.4 0.8 %copy.7 = f32[2,32,2,2,432]{4,3,2,1,0:T(2,128)} copy(f32[2,32,2,2,432]{4,3,2,1,0:T(2,128)S(1)} %bitcast.7) | data formatting | bytes 884736
Async XLA Ops:
  0.0 0.7 %copy-start.2 = (s32[32,3]{0,1:T(4,128)S(1)}, s32[32,3]{0,1:T(4,128)}, u32[]{:S(2)}) copy-start(s32[32,3]{0,1:T(4,128)} %param.9) | copy-start | bytes 1156
  0.0 0.7 %copy-start.1 = (s32[24,3]{0,1:T(4,128)S(1)}, s32[24,3]{0,1:T(4,128)}, u32[]{:S(2)}) copy-start(s32[24,3]{0,1:T(4,128)} %param.6) | copy-start | bytes 868
  0.0 0.7 %copy-start.3 = (s32[2,3]{1,0:T(2,128)S(1)}, s32[2,3]{1,0:T(2,128)}, u32[]{:S(2)}) copy-start(s32[2,3]{1,0:T(2,128)} %refs_0_.1) | copy-start | bytes 76
  0.0 0.7 %copy-start.4 = (s32[24]{0:T(128)S(1)}, s32[24]{0:T(128)}, u32[]{:S(2)}) copy-start(s32[24]{0:T(128)} %param.7) | copy-start | bytes 292
  0.7 1.0 %copy-start = (bf16[1,2,2,12,12,256]{5,2,4,3,1,0:T(2,128)(2,1)S(1)}, bf16[1,2,2,12,12,256]{5,2,4,3,1,0:T(2,128)(2,1)}, u32[]{:S(2)}) copy-start(bf16[1,2,2,12,12,256]{5,2,4,3,1,0:T(2,128)(2,1)} %param.5) | copy-start | bytes 884740
